TPU v7x, 32 devices: a whole 2x2x4 slice. The times are simulated.
32 devices in a mesh: seq: 8 (over y, x, core), tensor: 4 (over z).
Axes of the slice: x: 2, y: 2, z: 4, core: 2. Of those that a mesh axis runs over, the one named last changes fastest.
Arguments:
- tokens: bfloat16 [4096, 8192], P('seq', 'tensor'), may hold values from -6 to 6
- positions: int32 [4096], P('seq'), may hold values from 0 to 4095, each once
- norm_gain: float32 [8192], replicated, may hold values from 0.1 to 1.9
- w_query: bfloat16 [8192, 4096], P('seq', 'tensor'), may hold values from -0.0625 to 0.0625
- w_key: bfloat16 [8192, 1024], P('seq', 'tensor'), may hold values from -0.0625 to 0.0625
- w_value: bfloat16 [8192, 1024], P('seq', 'tensor'), may hold values from -0.0625 to 0.0625
- b_query: float32 [4096], P('tensor'), may hold values from -40 to 40
- b_key: float32 [1024], P('tensor'), may hold values from -40 to 40
- b_value: float32 [1024], P('tensor'), may hold values from -6 to 6
- w_out: bfloat16 [4096, 8192], P('tensor', 'seq'), may hold values from -0.09375 to 0.09375
Outputs:
- mixed: bfloat16 [4096, 8192], P('seq', 'tensor')
- context: bfloat16 [4096, 4096], P('seq', 'tensor')
Inputs may be any that keep to these rules, and one draw needn't show every extreme that they name: positions holds every position 0 to 4095 once.
All inputs are finite; a program needn't handle non-finite values.
Results may differ from a plain program's by a relative error of at most 0.025.
Values may be sent and summed in bfloat16 or wider, within the bound.
A program may use at most 128 MiB of HBM per device.

v0:
```python
import functools

import jax
import jax.numpy as jnp
from jax import lax
from jax.experimental import pallas as pl
from jax.experimental.pallas import tpu as pltpu
from jax.sharding import PartitionSpec as P

HD = 128


NORM_EPS = 1e-06
ROPE_BASE = 1000000.0
NEG_FILL = -1e30
CORES = 2
PAIR = 2
PLANE_SEMS = 10
MESH = pl.DeviceIdType.MESH
ANY = pl.BlockSpec(memory_space=pl.ANY)
VMEM = pl.BlockSpec(memory_space=pltpu.VMEM)


def plane_sems(n):
    chips = n // CORES
    return PLANE_SEMS if chips == 4 else 2 * chips


def plane_partners(n, s):
    twin = s + 1 - 2 * (s % CORES)
    chips = n // CORES
    if chips == 4:
        return [twin, s + 2 - 4 * ((s // 2) % 2), (s + 4) % n]
    return [twin] + [(s + CORES * j) % n for j in range(1, chips)]


def plane_gather(n, s, items, send_sem, recv_sem):
    twin = s + 1 - 2 * (s % CORES)
    chips = n // CORES

    def copy(item, sem, source, dest, target):
        return pltpu.make_async_remote_copy(
            src_ref=source,
            dst_ref=dest,
            send_sem=send_sem.at[item, sem],
            recv_sem=recv_sem.at[item, sem],
            device_id={"seq": target},
            device_id_type=MESH,
        )

    if chips == 4:
        xn = s + 2 - 4 * ((s // 2) % 2)
        yn = (s + 4) % n
        dg = (xn + 4) % n

        def half(ref, item, i):
            rows = items[item][2] // 2
            return ref.at[pl.ds(i * rows, rows), :]

        def piece(item, sem, block, i, target, own=False):
            source, slot, _ = items[item]
            dest = half(slot(block), item, i)
            return copy(item, sem, half(source, item, i) if own else dest, dest, target)

        def across(item, sem, block, own=False):
            source, slot, _ = items[item]
            return copy(item, sem, source if own else slot(block), slot(block), twin)

        def other(block):
            return block + 1 - 2 * (block % CORES)

        def start(item):
            piece(item, 0, s, 0, xn, True).start()
            piece(item, 3, s, 1, yn, True).start()
            piece(item, 1, s, 1, xn, True).start()
            piece(item, 2, s, 0, yn, True).start()
            across(item, 6, s, True).start()

        def relay(item, stage):
            if stage == 0:
                piece(item, 0, xn, 0, xn).wait_recv()
                piece(item, 4, xn, 0, yn).start()
                piece(item, 3, yn, 1, yn).wait_recv()
                piece(item, 5, yn, 1, xn).start()
            elif stage == 1:
                piece(item, 1, xn, 1, xn).wait_recv()
                across(item, 7, xn).start()
                piece(item, 2, yn, 0, yn).wait_recv()
                across(item, 8, yn).start()
            else:
                piece(item, 4, dg, 0, yn).wait_recv()
                piece(item, 5, dg, 1, xn).wait_recv()
                across(item, 9, dg).start()

        def finish(item):
            for sem, block in ((6, s), (7, xn), (8, yn), (9, dg)):
                across(item, sem, other(block)).wait_recv()

        def drain(item):
            piece(item, 0, s, 0, xn, True).wait_send()
            piece(item, 3, s, 1, yn, True).wait_send()
            piece(item, 1, s, 1, xn, True).wait_send()
            piece(item, 2, s, 0, yn, True).wait_send()
            piece(item, 4, xn, 0, yn).wait_send()
            piece(item, 5, yn, 1, xn).wait_send()
            across(item, 6, s, True).wait_send()
            for sem, block in ((7, xn), (8, yn), (9, dg)):
                across(item, sem, block).wait_send()

    else:

        def hop(item, kind, j, block, own, target):
            source, slot, _ = items[item]
            return copy(item, kind * chips + j, source if own else slot(block), slot(block), target)

        def start(item):
            for j in range(1, chips):
                hop(item, 0, j, s, True, (s + CORES * j) % n).start()
            hop(item, 1, 0, s, True, twin).start()

        def relay(item, stage):
            if stage == 2:
                for j in range(1, chips):
                    origin = (s + n - CORES * j) % n
                    hop(item, 0, j, origin, False, origin).wait_recv()
                    hop(item, 1, j, origin, False, twin).start()

        def finish(item):
            for j in range(chips):
                hop(item, 1, j, (twin + n - CORES * j) % n, False, twin).wait_recv()

        def drain(item):
            for j in range(1, chips):
                hop(item, 0, j, s, True, (s + CORES * j) % n).wait_send()
            hop(item, 1, 0, s, True, twin).wait_send()
            for j in range(1, chips):
                hop(item, 1, j, (s + n - CORES * j) % n, False, twin).wait_send()

    return start, relay, finish, drain


def line_sends(m, t, step):
    right = (t >= step) & (t < m - 1)
    left = (t + step < m) & (t > 0)
    return (right, 0, t - step, t + 1), (left, 1, t + step, t - 1)


def line_takes(m, t, step):
    return (
        (t - 1 - step >= 0, 0, t - 1 - step, t - 1),
        (t + 1 + step < m, 1, t + 1 + step, t + 1),
    )


def line_neighbours(m, t, act):
    @pl.when(t > 0)
    def _():
        act(t - 1)

    @pl.when(t < m - 1)
    def _():
        act(t + 1)


def project_kernel(
    n, m, tokens, w_query, w_key, w_value, w_out, gain, bias, cosine, sine, q, kv, w_mix,
    tok_all, wq_all, wkv_all, acc, squares, scaled,
    plane_send, plane_recv, line_send, line_recv, mix_send, mix_recv, local_sem,
):
    s = lax.axis_index("seq")
    t = lax.axis_index("tensor")
    heads, rows, _ = q.shape
    kv_heads = kv.shape[0]
    depth, query_cols = w_query.shape
    key_cols = w_key.shape[1]
    feats = tokens.shape[1]
    g = n // m
    part = s % g
    home = s // g
    piece_rows = w_out.shape[0] // m

    barrier = pltpu.get_barrier_semaphore()
    partners = plane_partners(n, s)
    for other in partners:
        pl.semaphore_signal(barrier, inc=1, device_id={"seq": other}, device_id_type=MESH)
    line_neighbours(
        m, t, lambda o: pl.semaphore_signal(barrier, inc=1, device_id={"tensor": o}, device_id_type=MESH)
    )
    for p in range(m):

        @pl.when(home != p)
        def _():
            pl.semaphore_signal(barrier, inc=1, device_id={"seq": g * p + part}, device_id_type=MESH)

    ends = jnp.where(t > 0, 1, 0) + jnp.where(t < m - 1, 1, 0)
    pl.semaphore_wait(barrier, len(partners) + ends + (m - 1))

    def wq_slot(b):
        return wq_all.at[pl.ds(pl.multiple_of(b * depth, 128), depth), :]

    def wk_slot(b):
        return wkv_all.at[pl.ds(pl.multiple_of(b * depth, 128), depth), pl.ds(0, key_cols)]

    def wv_slot(b):
        return wkv_all.at[pl.ds(pl.multiple_of(b * depth, 128), depth), pl.ds(key_cols, key_cols)]

    items = [(w_query, wq_slot, depth), (w_key, wk_slot, depth), (w_value, wv_slot, depth)]
    start, relay, finish, drain = plane_gather(n, s, items, plane_send, plane_recv)

    def line(way, step, block, first, target):
        return pltpu.make_async_remote_copy(
            src_ref=tokens if first else tok_all.at[block],
            dst_ref=tok_all.at[block],
            send_sem=line_send.at[way, step],
            recv_sem=line_recv.at[way, step],
            device_id={"tensor": target},
            device_id_type=MESH,
        )

    def send_line(step):
        for cond, way, block, target in line_sends(m, t, step):

            @pl.when(cond)
            def _():
                line(way, step, block, step == 0, target).start()

    def take_line(step):
        for valid, way, block, source in line_takes(m, t, step):

            @pl.when(valid)
            def _():
                line(way, step, block, False, source).wait_recv()

    send_line(0)
    for item in range(3):
        start(item)

    def mix(p):
        return pltpu.make_async_remote_copy(
            src_ref=w_out.at[pl.ds(p * piece_rows, piece_rows), :],
            dst_ref=w_mix.at[home],
            send_sem=mix_send.at[p],
            recv_sem=mix_recv.at[home],
            device_id={"seq": g * p + part},
            device_id_type=MESH,
        )

    def mixed_in(f):
        return pltpu.make_async_remote_copy(
            src_ref=w_mix.at[f],
            dst_ref=w_mix.at[f],
            send_sem=mix_send.at[f],
            recv_sem=mix_recv.at[f],
            device_id={"seq": g * f + part},
            device_id_type=MESH,
        )

    own = [
        pltpu.make_async_copy(tokens, tok_all.at[t], local_sem.at[0]),
        pltpu.make_async_copy(w_query, wq_slot(s), local_sem.at[1]),
        pltpu.make_async_copy(w_key, wk_slot(s), local_sem.at[2]),
        pltpu.make_async_copy(w_value, wv_slot(s), local_sem.at[3]),
    ]
    for copy in own:
        copy.start()
    acc[...] = jnp.zeros_like(acc)
    squares[...] = jnp.zeros_like(squares)

    for item in range(3):
        relay(item, 0)
    for p in range(m):

        @pl.when(home != p)
        def _():
            mix(p).start()

    step_of = 0
    for stage in (1, 2):
        if step_of < m - 1:
            take_line(step_of)
            step_of += 1
            if step_of < m - 1:
                send_line(step_of)
        for item in range(3):
            relay(item, stage)
    while step_of < m - 2:
        take_line(step_of)
        step_of += 1
        send_line(step_of)
    for copy in own:
        copy.wait()
    for item in range(3):
        finish(item)

    part_feats = depth
    parts = feats // part_feats

    def multiply(block):
        def one(i, _):
            at = pl.multiple_of(i * part_feats, 128)
            x = tok_all[block, :, pl.ds(at, part_feats)].astype(jnp.float32)
            sq = x * x
            total = sq[:, 0:128]
            for c in range(1, part_feats // 128):
                total = total + sq[:, c * 128 : (c + 1) * 128]
            squares[...] += total
            scaled[...] = (x * gain[block, :, pl.ds(at, part_feats)]).astype(jnp.bfloat16)
            row = pl.multiple_of(block * feats + at, 128)
            half = query_cols // 2
            for c in range(2):
                cols = slice(c * half, (c + 1) * half)
                acc[:, cols] += jnp.dot(
                    scaled[...], wq_all[pl.ds(row, part_feats), cols], preferred_element_type=jnp.float32
                )
            acc[:, query_cols:] += jnp.dot(
                scaled[...], wkv_all[pl.ds(row, part_feats), :], preferred_element_type=jnp.float32
            )
            return 0

        lax.fori_loop(0, parts, one, 0)

    multiply(t)
    for step in range(m - 1):
        if step == m - 2:
            take_line(step)
        for valid, _, block, _ in line_takes(m, t, step):

            @pl.when(valid)
            def _():
                multiply(block)

    mean = jnp.sum(squares[...], -1, keepdims=True) / (m * feats)
    inverse_rms = lax.rsqrt(mean + NORM_EPS)

    def head(i):
        cols = slice(i * HD, (i + 1) * HD)
        return acc[:, cols] * inverse_rms + bias[:, cols]

    def turned(i):
        value = head(i)
        return (value * cosine[...] + pltpu.roll(value, HD // 2, 1) * sine[...]).astype(jnp.bfloat16)

    for h in range(heads):
        q[h] = turned(h)
    for h in range(kv_heads):
        kv[h, :, 0:HD] = turned(heads + h)
        kv[h, :, HD : 2 * HD] = head(heads + kv_heads + h).astype(jnp.bfloat16)

    for item in range(3):
        drain(item)
    for p in range(m):

        @pl.when(home != p)
        def _():
            mix(p).wait_send()
            mixed_in(p).wait_recv()

    for step in range(m - 1):
        for cond, way, block, target in line_sends(m, t, step):

            @pl.when(cond)
            def _():
                line(way, step, block, step == 0, target).wait_send()


def project(n, m, tokens, w_query, w_key, w_value, w_out, gain, bias, cosine, sine):
    rows, feats = tokens.shape
    depth, query_cols = w_query.shape
    key_cols = w_key.shape[1]
    heads, kv_heads = query_cols // HD, key_cols // HD
    wrows, wcols = w_out.shape
    bf16, f32 = jnp.bfloat16, jnp.float32
    dma = pltpu.SemaphoreType.DMA
    return pl.pallas_call(
        functools.partial(project_kernel, n, m),
        out_shape=(
            jax.ShapeDtypeStruct((heads, rows, HD), bf16),
            jax.ShapeDtypeStruct((kv_heads, rows, 2 * HD), bf16),
            jax.ShapeDtypeStruct((m, wrows // m, wcols), bf16),
        ),
        in_specs=[ANY] * 5 + [VMEM] * 4,
        out_specs=(VMEM, VMEM, ANY),
        scratch_shapes=[
            pltpu.VMEM((m, rows, feats), bf16),
            pltpu.VMEM((n * depth, query_cols), bf16),
            pltpu.VMEM((n * depth, 2 * key_cols), bf16),
            pltpu.VMEM((rows, query_cols + 2 * key_cols), f32),
            pltpu.VMEM((rows, 128), f32),
            pltpu.VMEM((rows, depth), bf16),
            dma((3, plane_sems(n))),
            dma((3, plane_sems(n))),
            dma((2, m - 1)),
            dma((2, m - 1)),
            dma((m,)),
            dma((m,)),
            dma((4,)),
        ],
        compiler_params=pltpu.CompilerParams(
            collective_id=0, has_side_effects=True, vmem_limit_bytes=60 * 2**20
        ),
        cost_estimate=pl.CostEstimate(flops=10**11, bytes_accessed=10**8, transcendentals=0),
    )(tokens, w_query, w_key, w_value, w_out, gain, bias, cosine, sine)


def attend_kernel(
    n, m, q, kv, pos, qpos, tokens, w_out, w_mix, mixed, context,
    kv_all, pos_all, ctx_all, w_all, scores, biggest, total, acc, residual,
    plane_send, plane_recv, swap_send, swap_recv, line_send, line_recv, local_sem,
):
    s = lax.axis_index("seq")
    t = lax.axis_index("tensor")
    heads, rows, _ = q.shape
    kv_heads = kv.shape[0]
    group = heads // kv_heads
    g = n // m
    part = s % g
    home = s // g
    wrows, wcols = w_out.shape
    piece_rows = wrows // m
    chunks = heads // PAIR
    width = PAIR * HD
    outs = acc.shape[1]

    barrier = pltpu.get_barrier_semaphore()
    partners = plane_partners(n, s)
    for other in partners:
        pl.semaphore_signal(barrier, inc=1, device_id={"seq": other}, device_id_type=MESH)
    for other in range(m):

        @pl.when(t != other)
        def _():
            pl.semaphore_signal(barrier, inc=1, device_id={"tensor": other}, device_id_type=MESH)

    pl.semaphore_wait(barrier, len(partners) + m - 1)

    def kv_slot(h):
        return lambda b: kv_all.at[h, pl.ds(pl.multiple_of(b * rows, 128), rows), :]

    def w_slot(b, tt):
        return w_all.at[
            pl.ds(pl.multiple_of(tt * wrows + (b // g) * piece_rows, 16), piece_rows),
            pl.ds(pl.multiple_of((b % g) * wcols, 128), wcols),
        ]

    items = [(kv.at[h], kv_slot(h), rows) for h in range(kv_heads)]
    items.append((pos, lambda b: pos_all.at[b], pos.shape[0]))
    first_w = len(items)
    turn = 1 - 2 * (t // (m // 2))
    order = [(t + m + d * turn) % m for d in range(m)]
    for tt in order:
        items.append((w_slot(s, tt), lambda b, tt=tt: w_slot(b, tt), piece_rows))
    start, relay, finish, drain = plane_gather(n, s, items, plane_send, plane_recv)

    start(first_w - 1)
    for h in range(kv_heads):
        start(h)

    def swap(f, own):
        source = w_out.at[pl.ds(pl.multiple_of(home * piece_rows, 16), piece_rows), :]
        return pltpu.make_async_remote_copy(
            src_ref=source if own else w_mix.at[f],
            dst_ref=w_slot(s, t),
            send_sem=swap_send.at[f],
            recv_sem=swap_recv.at[t],
            device_id={"tensor": f},
            device_id_type=MESH,
        )

    def keep(own):
        source = w_out.at[pl.ds(pl.multiple_of(home * piece_rows, 16), piece_rows), :]
        return pltpu.make_async_copy(source if own else w_mix.at[t], w_slot(s, t), local_sem.at[0])

    for f in order[1:]:

        @pl.when(home == f)
        def _():
            swap(f, True).start()

        @pl.when(home != f)
        def _():
            swap(f, False).start()

    @pl.when(home == t)
    def _():
        keep(True).start()

    @pl.when(home != t)
    def _():
        keep(False).start()

    for h in range(kv_heads):
        kv_all[h, pl.ds(pl.multiple_of(s * rows, 128), rows), :] = kv[h]
    pos_all[s] = pos[...]

    load = pltpu.make_async_copy(tokens, residual, local_sem.at[1])
    load.start()

    def arrived(tt):
        pltpu.make_async_remote_copy(
            src_ref=w_slot(s, tt),
            dst_ref=w_slot(s, tt),
            send_sem=swap_send.at[tt],
            recv_sem=swap_recv.at[tt],
            device_id={"tensor": tt},
            device_id_type=MESH,
        ).wait_recv()

    def line(way, step, chunk, block, target):
        return pltpu.make_async_remote_copy(
            src_ref=ctx_all.at[block, chunk],
            dst_ref=ctx_all.at[block, chunk],
            send_sem=line_send.at[way, step, chunk],
            recv_sem=line_recv.at[way, step, chunk],
            device_id={"tensor": target},
            device_id_type=MESH,
        )

    def send_line(step, chunk):
        for cond, way, block, target in line_sends(m, t, step):

            @pl.when(cond)
            def _():
                line(way, step, chunk, block, target).start()

    query_pos = qpos[...]
    scale = HD ** (-0.5) * 1.4426950408889634

    def attend(h):
        base = h // group

        def block_scores(b, _):
            at = pl.multiple_of(b * rows, 128)
            keys = kv_all[base, pl.ds(at, rows), 0:HD]
            raw = lax.dot_general(
                q[h], keys, (((1,), (1,)), ((), ())), preferred_element_type=jnp.float32
            )
            masked = jnp.where(pos_all[b, 0:1, :] <= query_pos, raw, NEG_FILL)
            scores[b] = masked
            top = biggest[...]
            for i in range(rows // 128):
                top = jnp.maximum(top, masked[:, i * 128 : (i + 1) * 128])
            biggest[...] = top
            return 0

        biggest[...] = jnp.full_like(biggest, NEG_FILL)
        lax.fori_loop(0, n, block_scores, 0)
        row_max = jnp.max(biggest[...], -1, keepdims=True) * scale
        total[...] = jnp.zeros_like(total)
        biggest[...] = jnp.zeros_like(biggest)

        def block_values(b, _):
            at = pl.multiple_of(b * rows, 128)
            weights = jnp.exp2(scores[b] * scale - row_max)
            value = kv_all[base, pl.ds(at, rows), HD : 2 * HD]
            total[...] += jnp.dot(
                weights.astype(jnp.bfloat16), value, preferred_element_type=jnp.float32
            )
            add = weights[:, 0:128]
            for i in range(1, rows // 128):
                add = add + weights[:, i * 128 : (i + 1) * 128]
            biggest[...] += add
            return 0

        lax.fori_loop(0, n, block_values, 0)
        denominator = jnp.sum(biggest[...], -1, keepdims=True)
        return (total[...] / denominator).astype(jnp.bfloat16)

    for stage in range(3):
        relay(first_w - 1, stage)
        for h in range(kv_heads):
            relay(h, stage)
    keep(True).wait()
    start(first_w)
    finish(first_w - 1)

    work = []
    for d in range(1, m):
        work.append([("start", d), ("relay", d - 1, 0)])
        if d > 1:
            work[-1].append(("relay", d - 2, 1))
        if d > 2:
            work[-1].append(("relay", d - 3, 2))

    def advance(jobs):
        for job in jobs:
            if job[0] == "start":
                arrived(order[job[1]])
                start(first_w + job[1])
            else:
                relay(first_w + job[1], job[2])

    rest = []
    for d in range(m):
        for stage in range(3):
            if all(("relay", d, stage) not in jobs for jobs in work):
                rest.append((d + stage, d, ("relay", d, stage)))
    rest = [job for _, _, job in sorted(rest)]

    stored = []
    for chunk in range(chunks):
        base = chunk * PAIR // group
        if chunk * PAIR % group == 0:
            finish(base)

        def one(i, _):
            value = attend(chunk * PAIR + i)
            ctx_all[t, chunk, :, pl.ds(pl.multiple_of(i * HD, HD), HD)] = value
            return 0

        lax.fori_loop(0, PAIR, one, 0)
        send_line(0, chunk)
        out = pltpu.make_async_copy(
            ctx_all.at[t, chunk],
            context.at[:, pl.ds(chunk * width, width)],
            local_sem.at[2 + chunk],
        )
        out.start()
        stored.append(out)
        if chunk < len(work):
            advance(work[chunk])
    for jobs in work[chunks:]:
        advance(jobs)

    load.wait()

    def out_proj(block, first):
        for j in range(outs // wcols):
            cols = slice(j * wcols, (j + 1) * wcols)

            def partial(c):
                at = pl.multiple_of(block * wrows + c * width, 128)
                return jnp.dot(
                    ctx_all[block, c], w_all[pl.ds(at, width), cols], preferred_element_type=jnp.float32
                )

            value = partial(0)
            for c in range(1, chunks):
                value = value + partial(c)
            acc[:, cols] = value + (residual[:, cols].astype(jnp.float32) if first else acc[:, cols])

    def take_line(step):
        for valid, way, block, source in line_takes(m, t, step):
            for chunk in range(chunks):

                @pl.when(valid)
                def _():
                    line(way, step, chunk, block, source).wait_recv()

                if step + 1 < m - 1:
                    go = valid & ((t < m - 1) if way == 0 else (t > 0))
                    onward = t + 1 if way == 0 else t - 1

                    @pl.when(go)
                    def _():
                        line(way, step + 1, chunk, block, onward).start()

    def add_blocks(step):
        def way(i, _):
            block = jnp.where(i == 0, t - 1 - step, t + 1 + step)

            @pl.when((block >= 0) & (block < m))
            def _():
                out_proj(block, False)

            return 0

        lax.fori_loop(0, 2, way, 0)

    take_line(0)
    cut = (len(rest) + 1) // 2
    advance(rest[:cut])
    for step in range(1, m - 2):
        take_line(step)
    advance(rest[cut:])
    for d in range(m):
        finish(first_w + d)
    out_proj(t, True)
    for step in range(m - 1):
        if step == m - 2 and step > 0:
            take_line(step)
        add_blocks(step)

    residual[...] = acc[...].astype(jnp.bfloat16)
    final = pltpu.make_async_copy(residual, mixed, local_sem.at[1])
    final.start()

    for item in range(len(items)):
        drain(item)
    for f in order[1:]:
        swap(f, False).wait_send()

    for step in range(m - 1):
        for cond, way, block, target in line_sends(m, t, step):
            for chunk in range(chunks):

                @pl.when(cond)
                def _():
                    line(way, step, chunk, block, target).wait_send()

    for out in stored:
        out.wait()
    final.wait()


def attend_and_mix(n, m, q, kv, pos, qpos, tokens, w_out, w_mix):
    heads, rows, _ = q.shape
    kv_heads = kv.shape[0]
    wrows, wcols = w_out.shape
    outs = tokens.shape[1]
    chunks = heads // PAIR
    items = kv_heads + 1 + m
    bf16, f32 = jnp.bfloat16, jnp.float32
    dma = pltpu.SemaphoreType.DMA
    return pl.pallas_call(
        functools.partial(attend_kernel, n, m),
        out_shape=(
            jax.ShapeDtypeStruct(tokens.shape, bf16),
            jax.ShapeDtypeStruct((rows, heads * HD), bf16),
        ),
        in_specs=[VMEM, VMEM, VMEM, VMEM, ANY, ANY, ANY],
        out_specs=(ANY, ANY),
        scratch_shapes=[
            pltpu.VMEM((kv_heads, n * rows, 2 * HD), bf16),
            pltpu.VMEM((n, *pos.shape), pos.dtype),
            pltpu.VMEM((m, chunks, rows, PAIR * HD), bf16),
            pltpu.VMEM((m * wrows, outs), bf16),
            pltpu.VMEM((n, rows, rows), f32),
            pltpu.VMEM((rows, 128), f32),
            pltpu.VMEM((rows, HD), f32),
            pltpu.VMEM((rows, outs), f32),
            pltpu.VMEM((rows, outs), bf16),
            dma((items, plane_sems(n))),
            dma((items, plane_sems(n))),
            dma((m,)),
            dma((m,)),
            dma((2, m - 1, chunks)),
            dma((2, m - 1, chunks)),
            dma((2 + chunks,)),
        ],
        compiler_params=pltpu.CompilerParams(
            collective_id=1, has_side_effects=True, vmem_limit_bytes=60 * 2**20
        ),
        cost_estimate=pl.CostEstimate(flops=10**11, bytes_accessed=10**8, transcendentals=0),
    )(q, kv, pos, qpos, tokens, w_out, w_mix)


def shards(seq, tensor, tokens, positions, norm_gain, w_query, w_key, w_value, b_query, b_key, b_value, w_out):
    rows, feats = tokens.shape
    half = HD // 2
    inv_freq = ROPE_BASE ** (-jnp.arange(half, dtype=jnp.float32) * 2.0 / HD)
    inv_freq = jnp.concatenate((inv_freq, inv_freq))
    sign = jnp.where(jnp.arange(HD) < half, -1.0, 1.0)
    angles = positions.astype(jnp.float32)[:, None] * inv_freq[None, :]
    cosine = jnp.cos(angles)
    sine = jnp.sin(angles) * sign[None, :]
    bias = jnp.concatenate((b_query, b_key, b_value))[None, :]
    pos = jnp.broadcast_to(positions[None, :], (16, rows))
    q, kv, w_mix = project(
        seq, tensor, tokens, w_query, w_key, w_value, w_out,
        norm_gain.reshape(tensor, 1, feats), bias, cosine, sine,
    )
    return attend_and_mix(seq, tensor, q, kv, pos, positions[:, None], tokens, w_out, w_mix)


def solution(mesh):
    in_specs = (
        P("seq", "tensor"),
        P("seq"),
        P(),
        P("seq", "tensor"),
        P("seq", "tensor"),
        P("seq", "tensor"),
        P("tensor"),
        P("tensor"),
        P("tensor"),
        P("tensor", "seq"),
    )
    out_specs = (P("seq", "tensor"), P("seq", "tensor"))

    def body(*args):
        return shards(mesh.shape["seq"], mesh.shape["tensor"], *args)

    return jax.shard_map(body, mesh=mesh, in_specs=in_specs, out_specs=out_specs, check_vma=False)
```

profile of v0, /device:TPU:0, one launch (start us, length us, event | category | flops | bytes accessed | tf_op | source)
XLA Modules:
  0.0 305.3 jit_solution(10009838554449983601)
XLA Ops:
  0.6 0.1 compare_select_fusion
  0.7 0.7 convert_element_type.3
  1.4 0.7 pad_maximum_fusion
  2.1 0.6 broadcast_in_dim.23.bias
  2.7 1.3 broadcast_in_dim.26.pos
  4.0 1.5 copy.12.qpos
  5.6 1.8 fusion
  7.4 165.8 %shard_map.113 = (bf16[8,512,128]{2,1,0:T(8,128)(2,1)}, bf16[2,512,256]{2,1,0:T(8,128)(2,1)}, bf16[4,256,1024]{2,1,0:T(8,128)(2,1)}) custom-call(bf16[512,2048]{1,0:T(8,128)(2,1)} %tokens.3, bf16[1024,1024]{1,0:T(8,128)(2,1)} %w_query.1, bf16[1024,256]{1,0:T(8,128)(2,1)} %w_key.1, bf16[1024,256]{1,0:T(8,128)(2,1)} %w_value.1, bf16[1024,1024]{1,0:T(8,128)(2,1)} %w_out.3, ...), custom_call_target="tpu_custom_call" | custom-call | flops 99999997952 | bytes 100000000 | tf_op jit(solution)/shard_map/pallas_call | solution.py:374
  173.2 127.9 %shard_map.114 = (bf16[512,2048]{1,0:T(8,128)(2,1)}, bf16[512,1024]{1,0:T(8,128)(2,1)}) custom-call(bf16[8,512,128]{2,1,0:T(8,128)(2,1)} %get-tuple-element.5.q, bf16[2,512,256]{2,1,0:T(8,128)(2,1)} %get-tuple-element.6.kv, s32[16,512]{1,0:T(8,128)} %broadcast_in_dim.26.pos, s32[512,1]{1,0:T(8,128)} %copy.12.qpos, bf16[512,2048]{1,0:T(8,128)(2,1)} %tokens.3, ...), custom_call_target="tpu_custom_call" | custom-call | flops 99999997952 | bytes 100000000 | tf_op jit(solution)/shard_map/pallas_call | solution.py:714
  301.1 0.0 copy-start
  301.1 3.2 %copy.15 = bf16[512,2048]{1,0:T(8,128)(2,1)} copy(bf16[512,2048]{1,0:T(8,128)(2,1)} %get-tuple-element.14) | data formatting | bytes 4194304
  304.4 0.0 copy-done
  304.4 1.0 copy.16
  (1 shorter events, 0.0 us)
Async XLA Ops:
  301.1 3.3 %copy-start = (bf16[512,1024]{1,0:T(8,128)(2,1)S(1)}, bf16[512,1024]{1,0:T(8,128)(2,1)}, u32[]{:S(2)}) copy-start(bf16[512,1024]{1,0:T(8,128)(2,1)} %get-tuple-element.15) | copy-start | bytes 3145732
where the time goes:
time: 306 us; the launch traced here: 305 us
  Pallas kernels  294 us (96%)
  local copies, waits for them, and re-layouts  7.65 us (2%)
  other arithmetic  3.3 us (1%)
    pallas_call x1, Pallas kernels, project(): pl.pallas_call(functools.partial(project_kernel, n, m), out_shape=(jax.Sh...  166 us
    pallas_call x1, Pallas kernels, attend_and_mix(): pl.pallas_call(functools.partial(attend_kernel, n, m), out_shape=(jax.Sha...  128 us

commit v1 on v0

--- a/solution.py
+++ b/solution.py
@@ -69,12 +69,15 @@
         def other(block):
             return block + 1 - 2 * (block % CORES)
 
-        def start(item):
-            piece(item, 0, s, 0, xn, True).start()
-            piece(item, 3, s, 1, yn, True).start()
-            piece(item, 1, s, 1, xn, True).start()
-            piece(item, 2, s, 0, yn, True).start()
-            across(item, 6, s, True).start()
+        def start(*these):
+            for item in these:
+                piece(item, 0, s, 0, xn, True).start()
+                piece(item, 3, s, 1, yn, True).start()
+            for item in these:
+                piece(item, 1, s, 1, xn, True).start()
+                piece(item, 2, s, 0, yn, True).start()
+            for item in these:
+                across(item, 6, s, True).start()
 
         def relay(item, stage):
             if stage == 0:
@@ -92,9 +95,11 @@
                 piece(item, 5, dg, 1, xn).wait_recv()
                 across(item, 9, dg).start()
 
-        def finish(item):
-            for sem, block in ((6, s), (7, xn), (8, yn), (9, dg)):
+        def finish(item, near=True, far=True):
+            for sem, block in ((6, s), (7, xn), (8, yn)) if near else ():
                 across(item, sem, other(block)).wait_recv()
+            if far:
+                across(item, 9, other(dg)).wait_recv()
 
         def drain(item):
             piece(item, 0, s, 0, xn, True).wait_send()
@@ -113,10 +118,11 @@
             source, slot, _ = items[item]
             return copy(item, kind * chips + j, source if own else slot(block), slot(block), target)
 
-        def start(item):
-            for j in range(1, chips):
-                hop(item, 0, j, s, True, (s + CORES * j) % n).start()
-            hop(item, 1, 0, s, True, twin).start()
+        def start(*these):
+            for item in these:
+                for j in range(1, chips):
+                    hop(item, 0, j, s, True, (s + CORES * j) % n).start()
+                hop(item, 1, 0, s, True, twin).start()
 
         def relay(item, stage):
             if stage == 2:
@@ -125,8 +131,8 @@
                     hop(item, 0, j, origin, False, origin).wait_recv()
                     hop(item, 1, j, origin, False, twin).start()
 
-        def finish(item):
-            for j in range(chips):
+        def finish(item, near=True, far=True):
+            for j in range(chips) if far else ():
                 hop(item, 1, j, (twin + n - CORES * j) % n, False, twin).wait_recv()
 
         def drain(item):
@@ -163,8 +169,8 @@
 
 
 def project_kernel(
-    n, m, tokens, w_query, w_key, w_value, w_out, gain, bias, cosine, sine, q, kv, w_mix,
-    tok_all, wq_all, wkv_all, acc, squares, scaled,
+    n, m, tokens, w_query, w_key, w_value, w_out, gain, b_query, b_key, b_value, position, inv_freq,
+    q, kv, w_mix, cosine, sine, tok_all, wq_all, wkv_all, acc, squares, scaled,
     plane_send, plane_recv, line_send, line_recv, mix_send, mix_recv, local_sem,
 ):
     s = lax.axis_index("seq")
@@ -207,33 +213,39 @@
     items = [(w_query, wq_slot, depth), (w_key, wk_slot, depth), (w_value, wv_slot, depth)]
     start, relay, finish, drain = plane_gather(n, s, items, plane_send, plane_recv)
 
-    def line(way, step, block, first, target):
+    parts = feats // depth
+    chips = n // CORES
+
+    def late(block):
+        return block == chips - 1 - s // CORES if chips == 4 else block >= 0
+
+    def line(way, step, part_of, block, first, target):
         return pltpu.make_async_remote_copy(
-            src_ref=tokens if first else tok_all.at[block],
-            dst_ref=tok_all.at[block],
-            send_sem=line_send.at[way, step],
-            recv_sem=line_recv.at[way, step],
+            src_ref=tokens.at[:, pl.ds(part_of * depth, depth)] if first else tok_all.at[block, part_of],
+            dst_ref=tok_all.at[block, part_of],
+            send_sem=line_send.at[way, step, part_of],
+            recv_sem=line_recv.at[way, step, part_of],
             device_id={"tensor": target},
             device_id_type=MESH,
         )
 
-    def send_line(step):
+    def send_line(step, part_of):
         for cond, way, block, target in line_sends(m, t, step):
 
             @pl.when(cond)
             def _():
-                line(way, step, block, step == 0, target).start()
-
-    def take_line(step):
+                line(way, step, part_of, block, step == 0, target).start()
+
+    def take_line(step, part_of):
         for valid, way, block, source in line_takes(m, t, step):
 
             @pl.when(valid)
             def _():
-                line(way, step, block, False, source).wait_recv()
-
-    send_line(0)
-    for item in range(3):
-        start(item)
+                line(way, step, part_of, block, False, source).wait_recv()
+
+    for i in range(parts):
+        send_line(0, i)
+    start(0, 1, 2)
 
     def mix(p):
         return pltpu.make_async_remote_copy(
@@ -256,95 +268,122 @@
         )
 
     own = [
-        pltpu.make_async_copy(tokens, tok_all.at[t], local_sem.at[0]),
-        pltpu.make_async_copy(w_query, wq_slot(s), local_sem.at[1]),
-        pltpu.make_async_copy(w_key, wk_slot(s), local_sem.at[2]),
-        pltpu.make_async_copy(w_value, wv_slot(s), local_sem.at[3]),
+        pltpu.make_async_copy(w_query, wq_slot(s), local_sem.at[0]),
+        pltpu.make_async_copy(w_key, wk_slot(s), local_sem.at[1]),
+        pltpu.make_async_copy(w_value, wv_slot(s), local_sem.at[2]),
     ]
+    for i in range(parts):
+        own.append(
+            pltpu.make_async_copy(
+                tokens.at[:, pl.ds(i * depth, depth)], tok_all.at[t, i], local_sem.at[3 + i]
+            )
+        )
     for copy in own:
         copy.start()
     acc[...] = jnp.zeros_like(acc)
     squares[...] = jnp.zeros_like(squares)
 
+    def multiply(block, i):
+        x = tok_all[block, i].astype(jnp.float32)
+        sq = x * x
+        total = sq[:, 0:128]
+        for c in range(1, depth // 128):
+            total = total + sq[:, c * 128 : (c + 1) * 128]
+        squares[...] += total
+        scaled[...] = (x * gain[block, i]).astype(jnp.bfloat16)
+        row = pl.multiple_of(block * feats + i * depth, 128)
+        half = query_cols // 2
+        for c in range(2):
+            cols = slice(c * half, (c + 1) * half)
+            acc[:, cols] += jnp.dot(
+                scaled[...], wq_all[pl.ds(row, depth), cols], preferred_element_type=jnp.float32
+            )
+        acc[:, query_cols:] += jnp.dot(
+            scaled[...], wkv_all[pl.ds(row, depth), :], preferred_element_type=jnp.float32
+        )
+
+    def multiply_each(count, block_of, wanted):
+        def one(i, _):
+            block = block_of(i // parts)
+
+            @pl.when((block >= 0) & (block < m) & wanted(block))
+            def _():
+                multiply(block, i % parts)
+
+            return 0
+
+        lax.fori_loop(0, count * parts, one, 0)
+
+    place = position[...].astype(jnp.float32)
+    angles = jnp.transpose(jnp.broadcast_to(place, (HD, rows))) * inv_freq[...]
+    lane = lax.broadcasted_iota(jnp.int32, (rows, HD), 1)
+    cosine[...] = jnp.cos(angles)
+    turn = jnp.sin(angles)
+    sine[...] = jnp.where(lane < HD // 2, -turn, turn)
+
+    relay(0, 0)
+    for i in range(parts):
+        take_line(0, i)
+        if m > 2:
+            send_line(1, i)
+        if i == 0:
+            relay(1, 0)
+            relay(2, 0)
     for item in range(3):
-        relay(item, 0)
+        relay(item, 1)
+    for step in range(1, m - 2):
+        for i in range(parts):
+            take_line(step, i)
+            send_line(step + 1, i)
     for p in range(m):
 
         @pl.when(home != p)
         def _():
             mix(p).start()
 
-    step_of = 0
-    for stage in (1, 2):
-        if step_of < m - 1:
-            take_line(step_of)
-            step_of += 1
-            if step_of < m - 1:
-                send_line(step_of)
-        for item in range(3):
-            relay(item, stage)
-    while step_of < m - 2:
-        take_line(step_of)
-        step_of += 1
-        send_line(step_of)
     for copy in own:
         copy.wait()
     for item in range(3):
-        finish(item)
-
-    part_feats = depth
-    parts = feats // part_feats
-
-    def multiply(block):
-        def one(i, _):
-            at = pl.multiple_of(i * part_feats, 128)
-            x = tok_all[block, :, pl.ds(at, part_feats)].astype(jnp.float32)
-            sq = x * x
-            total = sq[:, 0:128]
-            for c in range(1, part_feats // 128):
-                total = total + sq[:, c * 128 : (c + 1) * 128]
-            squares[...] += total
-            scaled[...] = (x * gain[block, :, pl.ds(at, part_feats)]).astype(jnp.bfloat16)
-            row = pl.multiple_of(block * feats + at, 128)
-            half = query_cols // 2
-            for c in range(2):
-                cols = slice(c * half, (c + 1) * half)
-                acc[:, cols] += jnp.dot(
-                    scaled[...], wq_all[pl.ds(row, part_feats), cols], preferred_element_type=jnp.float32
-                )
-            acc[:, query_cols:] += jnp.dot(
-                scaled[...], wkv_all[pl.ds(row, part_feats), :], preferred_element_type=jnp.float32
-            )
+        finish(item, far=False)
+
+    def inside(block):
+        return (block - t < m - 1) & (t - block < m - 1)
+
+    multiply_each(m, lambda i: i, lambda b: jnp.logical_not(late(b)) & inside(b))
+    for item in range(3):
+        relay(item, 2)
+    for item in range(3):
+        finish(item, near=False)
+    multiply_each(m, lambda i: i, lambda b: late(b) & inside(b))
+    for i in range(parts):
+        take_line(m - 2, i)
+
+        def end(way, _):
+            block = t + (2 * way - 1) * (m - 1)
+
+            @pl.when((block >= 0) & (block < m))
+            def _():
+                multiply(block, i)
+
             return 0
 
-        lax.fori_loop(0, parts, one, 0)
-
-    multiply(t)
-    for step in range(m - 1):
-        if step == m - 2:
-            take_line(step)
-        for valid, _, block, _ in line_takes(m, t, step):
-
-            @pl.when(valid)
-            def _():
-                multiply(block)
+        lax.fori_loop(0, 2, end, 0)
 
     mean = jnp.sum(squares[...], -1, keepdims=True) / (m * feats)
     inverse_rms = lax.rsqrt(mean + NORM_EPS)
 
-    def head(i):
-        cols = slice(i * HD, (i + 1) * HD)
-        return acc[:, cols] * inverse_rms + bias[:, cols]
-
-    def turned(i):
-        value = head(i)
+    def head(i, bias, of):
+        return acc[:, i * HD : (i + 1) * HD] * inverse_rms + bias[:, of * HD : (of + 1) * HD]
+
+    def turned(i, bias, of):
+        value = head(i, bias, of)
         return (value * cosine[...] + pltpu.roll(value, HD // 2, 1) * sine[...]).astype(jnp.bfloat16)
 
     for h in range(heads):
-        q[h] = turned(h)
+        q[h] = turned(h, b_query, h)
     for h in range(kv_heads):
-        kv[h, :, 0:HD] = turned(heads + h)
-        kv[h, :, HD : 2 * HD] = head(heads + kv_heads + h).astype(jnp.bfloat16)
+        kv[h, :, 0:HD] = turned(heads + h, b_key, h)
+        kv[h, :, HD : 2 * HD] = head(heads + kv_heads + h, b_value, h).astype(jnp.bfloat16)
 
     for item in range(3):
         drain(item)
@@ -360,14 +399,16 @@
 
             @pl.when(cond)
             def _():
-                line(way, step, block, step == 0, target).wait_send()
-
-
-def project(n, m, tokens, w_query, w_key, w_value, w_out, gain, bias, cosine, sine):
+                for i in range(parts):
+                    line(way, step, i, block, step == 0, target).wait_send()
+
+
+def project(n, m, tokens, w_query, w_key, w_value, w_out, *small):
     rows, feats = tokens.shape
     depth, query_cols = w_query.shape
     key_cols = w_key.shape[1]
     heads, kv_heads = query_cols // HD, key_cols // HD
+    parts = feats // depth
     wrows, wcols = w_out.shape
     bf16, f32 = jnp.bfloat16, jnp.float32
     dma = pltpu.SemaphoreType.DMA
@@ -378,10 +419,12 @@
             jax.ShapeDtypeStruct((kv_heads, rows, 2 * HD), bf16),
             jax.ShapeDtypeStruct((m, wrows // m, wcols), bf16),
         ),
-        in_specs=[ANY] * 5 + [VMEM] * 4,
+        in_specs=[ANY] * 5 + [VMEM] * 6,
         out_specs=(VMEM, VMEM, ANY),
         scratch_shapes=[
-            pltpu.VMEM((m, rows, feats), bf16),
+            pltpu.VMEM((rows, HD), f32),
+            pltpu.VMEM((rows, HD), f32),
+            pltpu.VMEM((m, parts, rows, depth), bf16),
             pltpu.VMEM((n * depth, query_cols), bf16),
             pltpu.VMEM((n * depth, 2 * key_cols), bf16),
             pltpu.VMEM((rows, query_cols + 2 * key_cols), f32),
@@ -389,21 +432,21 @@
             pltpu.VMEM((rows, depth), bf16),
             dma((3, plane_sems(n))),
             dma((3, plane_sems(n))),
-            dma((2, m - 1)),
-            dma((2, m - 1)),
+            dma((2, m - 1, parts)),
+            dma((2, m - 1, parts)),
             dma((m,)),
             dma((m,)),
-            dma((4,)),
+            dma((3 + parts,)),
         ],
         compiler_params=pltpu.CompilerParams(
             collective_id=0, has_side_effects=True, vmem_limit_bytes=60 * 2**20
         ),
         cost_estimate=pl.CostEstimate(flops=10**11, bytes_accessed=10**8, transcendentals=0),
-    )(tokens, w_query, w_key, w_value, w_out, gain, bias, cosine, sine)
+    )(tokens, w_query, w_key, w_value, w_out, *small)
 
 
 def attend_kernel(
-    n, m, q, kv, pos, qpos, tokens, w_out, w_mix, mixed, context,
+    n, m, q, kv, pos, tokens, w_out, w_mix, mixed, context,
     kv_all, pos_all, ctx_all, w_all, scores, biggest, total, acc, residual,
     plane_send, plane_recv, swap_send, swap_recv, line_send, line_recv, local_sem,
 ):
@@ -522,7 +565,8 @@
             def _():
                 line(way, step, chunk, block, target).start()
 
-    query_pos = qpos[...]
+    mine = jnp.broadcast_to(pos[0:1, :].astype(jnp.float32), (128, rows))
+    query_pos = jnp.transpose(mine)[:, 0:1].astype(jnp.int32)
     scale = HD ** (-0.5) * 1.4426950408889634
 
     def attend(h):
@@ -567,8 +611,9 @@
 
     for stage in range(3):
         relay(first_w - 1, stage)
-        for h in range(kv_heads):
-            relay(h, stage)
+        relay(0, stage)
+    for h in range(1, kv_heads):
+        relay(h, 0)
     keep(True).wait()
     start(first_w)
     finish(first_w - 1)
@@ -595,6 +640,26 @@
             if all(("relay", d, stage) not in jobs for jobs in work):
                 rest.append((d + stage, d, ("relay", d, stage)))
     rest = [job for _, _, job in sorted(rest)]
+
+    def take_line(step, chunk):
+        for valid, way, block, source in line_takes(m, t, step):
+
+            @pl.when(valid)
+            def _():
+                line(way, step, chunk, block, source).wait_recv()
+
+            if step + 1 < m - 1:
+                go = valid & ((t < m - 1) if way == 0 else (t > 0))
+                onward = t + 1 if way == 0 else t - 1
+
+                @pl.when(go)
+                def _():
+                    line(way, step + 1, chunk, block, onward).start()
+
+    takes = [[] for _ in range(chunks + m)]
+    for step in range(m - 2):
+        for chunk in range(chunks):
+            takes[chunk + step + 1].append((step, chunk))
 
     stored = []
     for chunk in range(chunks):
@@ -616,6 +681,11 @@
         )
         out.start()
         stored.append(out)
+        for take in takes[chunk]:
+            take_line(*take)
+        if chunk * PAIR % group == 0 and base + 1 < kv_heads:
+            relay(base + 1, 1)
+            relay(base + 1, 2)
         if chunk < len(work):
             advance(work[chunk])
     for jobs in work[chunks:]:
@@ -638,22 +708,6 @@
                 value = value + partial(c)
             acc[:, cols] = value + (residual[:, cols].astype(jnp.float32) if first else acc[:, cols])
 
-    def take_line(step):
-        for valid, way, block, source in line_takes(m, t, step):
-            for chunk in range(chunks):
-
-                @pl.when(valid)
-                def _():
-                    line(way, step, chunk, block, source).wait_recv()
-
-                if step + 1 < m - 1:
-                    go = valid & ((t < m - 1) if way == 0 else (t > 0))
-                    onward = t + 1 if way == 0 else t - 1
-
-                    @pl.when(go)
-                    def _():
-                        line(way, step + 1, chunk, block, onward).start()
-
     def add_blocks(step):
         def way(i, _):
             block = jnp.where(i == 0, t - 1 - step, t + 1 + step)
@@ -666,18 +720,19 @@
 
         lax.fori_loop(0, 2, way, 0)
 
-    take_line(0)
-    cut = (len(rest) + 1) // 2
-    advance(rest[:cut])
-    for step in range(1, m - 2):
-        take_line(step)
-    advance(rest[cut:])
+    ahead = takes[chunks:]
+    per = (len(rest) + len(ahead) - 1) // len(ahead)
+    for i, group_of in enumerate(ahead):
+        for take in group_of:
+            take_line(*take)
+        advance(rest[i * per : (i + 1) * per])
     for d in range(m):
         finish(first_w + d)
     out_proj(t, True)
     for step in range(m - 1):
-        if step == m - 2 and step > 0:
-            take_line(step)
+        if step == m - 2:
+            for chunk in range(chunks):
+                take_line(step, chunk)
         add_blocks(step)
 
     residual[...] = acc[...].astype(jnp.bfloat16)
@@ -702,7 +757,7 @@
     final.wait()
 
 
-def attend_and_mix(n, m, q, kv, pos, qpos, tokens, w_out, w_mix):
+def attend_and_mix(n, m, q, kv, pos, tokens, w_out, w_mix):
     heads, rows, _ = q.shape
     kv_heads = kv.shape[0]
     wrows, wcols = w_out.shape
@@ -717,7 +772,7 @@
             jax.ShapeDtypeStruct(tokens.shape, bf16),
             jax.ShapeDtypeStruct((rows, heads * HD), bf16),
         ),
-        in_specs=[VMEM, VMEM, VMEM, VMEM, ANY, ANY, ANY],
+        in_specs=[VMEM, VMEM, VMEM, ANY, ANY, ANY],
         out_specs=(ANY, ANY),
         scratch_shapes=[
             pltpu.VMEM((kv_heads, n * rows, 2 * HD), bf16),
@@ -741,7 +796,7 @@
             collective_id=1, has_side_effects=True, vmem_limit_bytes=60 * 2**20
         ),
         cost_estimate=pl.CostEstimate(flops=10**11, bytes_accessed=10**8, transcendentals=0),
-    )(q, kv, pos, qpos, tokens, w_out, w_mix)
+    )(q, kv, pos, tokens, w_out, w_mix)
 
 
 def shards(seq, tensor, tokens, positions, norm_gain, w_query, w_key, w_value, b_query, b_key, b_value, w_out):
@@ -749,17 +804,13 @@
     half = HD // 2
     inv_freq = ROPE_BASE ** (-jnp.arange(half, dtype=jnp.float32) * 2.0 / HD)
     inv_freq = jnp.concatenate((inv_freq, inv_freq))
-    sign = jnp.where(jnp.arange(HD) < half, -1.0, 1.0)
-    angles = positions.astype(jnp.float32)[:, None] * inv_freq[None, :]
-    cosine = jnp.cos(angles)
-    sine = jnp.sin(angles) * sign[None, :]
-    bias = jnp.concatenate((b_query, b_key, b_value))[None, :]
     pos = jnp.broadcast_to(positions[None, :], (16, rows))
     q, kv, w_mix = project(
         seq, tensor, tokens, w_query, w_key, w_value, w_out,
-        norm_gain.reshape(tensor, 1, feats), bias, cosine, sine,
+        norm_gain.reshape(tensor, feats // w_query.shape[0], 1, w_query.shape[0]),
+        b_query[None, :], b_key[None, :], b_value[None, :], positions[None, :], inv_freq[None, :],
     )
-    return attend_and_mix(seq, tensor, q, kv, pos, positions[:, None], tokens, w_out, w_mix)
+    return attend_and_mix(seq, tensor, q, kv, pos, tokens, w_out, w_mix)
 
 
 def solution(mesh):

time: 306 us -> 282 us (0.922)
  Pallas kernels: 294 us -> 274 us
    pallas_call x1, Pallas kernels: 166 us -> 147 us  [project(): pl.pallas_call(functools.partial(project_kernel, n, m), out_shape=(jax.Sh...]
where the time goes in v1:
time: 282 us; the launch traced here: 280 us
  Pallas kernels  274 us (97%)
  local copies, waits for them, and re-layouts  5.52 us (2%)
    pallas_call x1, Pallas kernels, project(): pl.pallas_call(functools.partial(project_kernel, n, m), out_shape=(jax.Sh...  147 us
    pallas_call x1, Pallas kernels, attend_and_mix(): pl.pallas_call(functools.partial(attend_kernel, n, m), out_shape=(jax.Sha...  127 us

profile of v1, /device:TPU:0, one launch (start us, length us, event | category | flops | bytes accessed | tf_op | source)
XLA Modules:
  0.0 280.3 jit_solution(2929012699225373530)
XLA Ops:
  0.6 0.6 maximum_bitcast_fusion.inv_freq
  1.2 1.3 broadcast_in_dim.26.pos
  2.5 146.5 %shard_map.113 = (bf16[8,512,128]{2,1,0:T(8,128)(2,1)}, bf16[2,512,256]{2,1,0:T(8,128)(2,1)}, bf16[4,256,1024]{2,1,0:T(8,128)(2,1)}) custom-call(bf16[512,2048]{1,0:T(8,128)(2,1)} %tokens.3, bf16[1024,1024]{1,0:T(8,128)(2,1)} %w_query.1, bf16[1024,256]{1,0:T(8,128)(2,1)} %w_key.1, bf16[1024,256]{1,0:T(8,128)(2,1)} %w_value.1, bf16[1024,1024]{1,0:T(8,128)(2,1)} %w_out.3, ...), custom_call_target="tpu_custom_call" | custom-call | flops 99999997952 | bytes 100000000 | tf_op jit(solution)/shard_map/pallas_call | solution.py:415
  149.1 127.0 %shard_map.114 = (bf16[512,2048]{1,0:T(8,128)(2,1)}, bf16[512,1024]{1,0:T(8,128)(2,1)}) custom-call(bf16[8,512,128]{2,1,0:T(8,128)(2,1)} %get-tuple-element.5.q, bf16[2,512,256]{2,1,0:T(8,128)(2,1)} %get-tuple-element.6.kv, s32[16,512]{1,0:T(8,128)} %broadcast_in_dim.26.pos, bf16[512,2048]{1,0:T(8,128)(2,1)} %tokens.3, bf16[1024,1024]{1,0:T(8,128)(2,1)} %w_out.3, ...), custom_call_target="tpu_custom_call" | custom-call | flops 99999997952 | bytes 100000000 | tf_op jit(solution)/shard_map/pallas_call | solution.py:769
  276.1 0.0 copy-start
  276.1 3.2 %copy.14 = bf16[512,2048]{1,0:T(8,128)(2,1)} copy(bf16[512,2048]{1,0:T(8,128)(2,1)} %get-tuple-element.10) | data formatting | bytes 4194304
  279.4 0.0 copy-done
  279.4 1.0 copy.15
  (1 shorter events, 0.0 us)
Async XLA Ops:
  276.1 3.3 %copy-start = (bf16[512,1024]{1,0:T(8,128)(2,1)S(1)}, bf16[512,1024]{1,0:T(8,128)(2,1)}, u32[]{:S(2)}) copy-start(bf16[512,1024]{1,0:T(8,128)(2,1)} %get-tuple-element.11) | copy-start | bytes 3145732

commit v2 on v1

--- a/solution.py
+++ b/solution.py
@@ -14,7 +14,6 @@
 ROPE_BASE = 1000000.0
 NEG_FILL = -1e30
 CORES = 2
-PAIR = 2
 PLANE_SEMS = 10
 MESH = pl.DeviceIdType.MESH
 ANY = pl.BlockSpec(memory_space=pl.ANY)
@@ -170,8 +169,8 @@
 
 def project_kernel(
     n, m, tokens, w_query, w_key, w_value, w_out, gain, b_query, b_key, b_value, position, inv_freq,
-    q, kv, w_mix, cosine, sine, tok_all, wq_all, wkv_all, acc, squares, scaled,
-    plane_send, plane_recv, line_send, line_recv, mix_send, mix_recv, local_sem,
+    q, kv, w_mix, w_near, cosine, sine, tok_all, wq_all, wkv_all, acc, squares, scaled,
+    plane_send, plane_recv, line_send, line_recv, mix_send, mix_recv, near_send, near_recv, local_sem,
 ):
     s = lax.axis_index("seq")
     t = lax.axis_index("tensor")
@@ -355,6 +354,36 @@
     for item in range(3):
         finish(item, near=False)
     multiply_each(m, lambda i: i, lambda b: late(b) & inside(b))
+    for p in range(m):
+
+        @pl.when(home != p)
+        def _():
+            mixed_in(p).wait_recv()
+
+    inner = (t > 0) & (t < m - 1)
+    def near(way, own):
+        to = t + 1 - 2 * way
+        source = w_out.at[pl.ds(pl.multiple_of(home * piece_rows, 16), piece_rows), :]
+        return pltpu.make_async_remote_copy(
+            src_ref=source if own else w_mix.at[to],
+            dst_ref=w_near.at[way],
+            send_sem=near_send.at[way],
+            recv_sem=near_recv.at[way],
+            device_id={"tensor": to},
+            device_id_type=MESH,
+        )
+
+    sides = ((0, t < m - 2, inner), (1, t > 1, inner))
+    for way, gives, _ in sides:
+
+        @pl.when(gives & (home == t + 1 - 2 * way))
+        def _():
+            near(way, True).start()
+
+        @pl.when(gives & (home != t + 1 - 2 * way))
+        def _():
+            near(way, False).start()
+
     for i in range(parts):
         take_line(m - 2, i)
 
@@ -392,7 +421,23 @@
         @pl.when(home != p)
         def _():
             mix(p).wait_send()
-            mixed_in(p).wait_recv()
+
+    for way, gives, gets in sides:
+
+        @pl.when(gives)
+        def _():
+            near(way, True).wait_send()
+
+        @pl.when(gets)
+        def _():
+            pltpu.make_async_remote_copy(
+                src_ref=w_near.at[way],
+                dst_ref=w_near.at[way],
+                send_sem=near_send.at[way],
+                recv_sem=near_recv.at[way],
+                device_id={"tensor": t - 1 + 2 * way},
+                device_id_type=MESH,
+            ).wait_recv()
 
     for step in range(m - 1):
         for cond, way, block, target in line_sends(m, t, step):
@@ -418,9 +463,10 @@
             jax.ShapeDtypeStruct((heads, rows, HD), bf16),
             jax.ShapeDtypeStruct((kv_heads, rows, 2 * HD), bf16),
             jax.ShapeDtypeStruct((m, wrows // m, wcols), bf16),
+            jax.ShapeDtypeStruct((2, wrows // m, wcols), bf16),
         ),
         in_specs=[ANY] * 5 + [VMEM] * 6,
-        out_specs=(VMEM, VMEM, ANY),
+        out_specs=(VMEM, VMEM, ANY, ANY),
         scratch_shapes=[
             pltpu.VMEM((rows, HD), f32),
             pltpu.VMEM((rows, HD), f32),
@@ -436,6 +482,8 @@
             dma((2, m - 1, parts)),
             dma((m,)),
             dma((m,)),
+            dma((2,)),
+            dma((2,)),
             dma((3 + parts,)),
         ],
         compiler_params=pltpu.CompilerParams(
@@ -446,9 +494,9 @@
 
 
 def attend_kernel(
-    n, m, q, kv, pos, tokens, w_out, w_mix, mixed, context,
+    n, m, q, kv, pos, tokens, w_out, w_mix, w_near, mixed, context,
     kv_all, pos_all, ctx_all, w_all, scores, biggest, total, acc, residual,
-    plane_send, plane_recv, swap_send, swap_recv, line_send, line_recv, local_sem,
+    plane_send, plane_recv, swap_send, swap_recv, line_send, line_recv, near_sem, local_sem,
 ):
     s = lax.axis_index("seq")
     t = lax.axis_index("tensor")
@@ -460,8 +508,6 @@
     home = s // g
     wrows, wcols = w_out.shape
     piece_rows = wrows // m
-    chunks = heads // PAIR
-    width = PAIR * HD
     outs = acc.shape[1]
 
     barrier = pltpu.get_barrier_semaphore()
@@ -513,15 +559,31 @@
         source = w_out.at[pl.ds(pl.multiple_of(home * piece_rows, 16), piece_rows), :]
         return pltpu.make_async_copy(source if own else w_mix.at[t], w_slot(s, t), local_sem.at[0])
 
+    def beside(way):
+        return pltpu.make_async_copy(w_near.at[way], w_slot(s, t - 1 + 2 * way), near_sem.at[way])
+
+    inner = (t > 0) & (t < m - 1)
+
+    def apart(f):
+        return (f - t > 1) | (t - f > 1)
+
+    def far(f):
+        return apart(f) | (f == 0) | (f == m - 1)
+
     for f in order[1:]:
 
-        @pl.when(home == f)
+        @pl.when(far(f) & (home == f))
         def _():
             swap(f, True).start()
 
-        @pl.when(home != f)
+        @pl.when(far(f) & (home != f))
         def _():
             swap(f, False).start()
+
+    @pl.when(inner)
+    def _():
+        beside(0).start()
+        beside(1).start()
 
     @pl.when(home == t)
     def _():
@@ -539,19 +601,29 @@
     load.start()
 
     def arrived(tt):
-        pltpu.make_async_remote_copy(
-            src_ref=w_slot(s, tt),
-            dst_ref=w_slot(s, tt),
-            send_sem=swap_send.at[tt],
-            recv_sem=swap_recv.at[tt],
-            device_id={"tensor": tt},
-            device_id_type=MESH,
-        ).wait_recv()
+        @pl.when(inner & (tt == t - 1))
+        def _():
+            beside(0).wait()
+
+        @pl.when(inner & (tt == t + 1))
+        def _():
+            beside(1).wait()
+
+        @pl.when(apart(tt) | jnp.logical_not(inner))
+        def _():
+            pltpu.make_async_remote_copy(
+                src_ref=w_slot(s, tt),
+                dst_ref=w_slot(s, tt),
+                send_sem=swap_send.at[tt],
+                recv_sem=swap_recv.at[tt],
+                device_id={"tensor": tt},
+                device_id_type=MESH,
+            ).wait_recv()
 
     def line(way, step, chunk, block, target):
         return pltpu.make_async_remote_copy(
-            src_ref=ctx_all.at[block, chunk],
-            dst_ref=ctx_all.at[block, chunk],
+            src_ref=ctx_all.at[block, :, pl.ds(chunk * HD, HD)],
+            dst_ref=ctx_all.at[block, :, pl.ds(chunk * HD, HD)],
             send_sem=line_send.at[way, step, chunk],
             recv_sem=line_recv.at[way, step, chunk],
             device_id={"tensor": target},
@@ -618,28 +690,31 @@
     start(first_w)
     finish(first_w - 1)
 
-    work = []
-    for d in range(1, m):
-        work.append([("start", d), ("relay", d - 1, 0)])
-        if d > 1:
-            work[-1].append(("relay", d - 2, 1))
-        if d > 2:
-            work[-1].append(("relay", d - 3, 2))
+    ready = {d: 2 * d - 2 for d in range(1, m)}
+    due = [[] for _ in range(heads + 2 * m + 4)]
+    for chunk in range(heads):
+        for step in range(m - 2):
+            due[chunk + 1 + step].append((0, step, chunk))
+    for d in range(m):
+        if d:
+            due[ready[d]].append((1, d))
+        for stage in range(3):
+            due[ready.get(d, -1) + 1 + stage].append((2, d, stage))
+    for h in range(1, kv_heads):
+        for stage in (1, 2):
+            due[(h - 1) * group + stage - 1].append((3, h, stage))
 
     def advance(jobs):
-        for job in jobs:
-            if job[0] == "start":
+        for job in sorted(jobs):
+            if job[0] == 0:
+                take_line(*job[1:])
+            elif job[0] == 1:
                 arrived(order[job[1]])
                 start(first_w + job[1])
+            elif job[0] == 2:
+                relay(first_w + job[1], job[2])
             else:
-                relay(first_w + job[1], job[2])
-
-    rest = []
-    for d in range(m):
-        for stage in range(3):
-            if all(("relay", d, stage) not in jobs for jobs in work):
-                rest.append((d + stage, d, ("relay", d, stage)))
-    rest = [job for _, _, job in sorted(rest)]
+                relay(job[1], job[2])
 
     def take_line(step, chunk):
         for valid, way, block, source in line_takes(m, t, step):
@@ -656,40 +731,20 @@
                 def _():
                     line(way, step + 1, chunk, block, onward).start()
 
-    takes = [[] for _ in range(chunks + m)]
-    for step in range(m - 2):
-        for chunk in range(chunks):
-            takes[chunk + step + 1].append((step, chunk))
-
     stored = []
-    for chunk in range(chunks):
-        base = chunk * PAIR // group
-        if chunk * PAIR % group == 0:
-            finish(base)
-
-        def one(i, _):
-            value = attend(chunk * PAIR + i)
-            ctx_all[t, chunk, :, pl.ds(pl.multiple_of(i * HD, HD), HD)] = value
-            return 0
-
-        lax.fori_loop(0, PAIR, one, 0)
-        send_line(0, chunk)
+    for h in range(heads):
+        if h % group == 0:
+            finish(h // group)
+        ctx_all[t, :, h * HD : (h + 1) * HD] = attend(h)
+        send_line(0, h)
         out = pltpu.make_async_copy(
-            ctx_all.at[t, chunk],
-            context.at[:, pl.ds(chunk * width, width)],
-            local_sem.at[2 + chunk],
+            ctx_all.at[t, :, pl.ds(h * HD, HD)],
+            context.at[:, pl.ds(h * HD, HD)],
+            local_sem.at[2 + h],
         )
         out.start()
         stored.append(out)
-        for take in takes[chunk]:
-            take_line(*take)
-        if chunk * PAIR % group == 0 and base + 1 < kv_heads:
-            relay(base + 1, 1)
-            relay(base + 1, 2)
-        if chunk < len(work):
-            advance(work[chunk])
-    for jobs in work[chunks:]:
-        advance(jobs)
+        advance(due[h])
 
     load.wait()
 
@@ -697,15 +752,10 @@
         for j in range(outs // wcols):
             cols = slice(j * wcols, (j + 1) * wcols)
 
-            def partial(c):
-                at = pl.multiple_of(block * wrows + c * width, 128)
-                return jnp.dot(
-                    ctx_all[block, c], w_all[pl.ds(at, width), cols], preferred_element_type=jnp.float32
-                )
-
-            value = partial(0)
-            for c in range(1, chunks):
-                value = value + partial(c)
+            at = pl.multiple_of(block * wrows, 128)
+            value = jnp.dot(
+                ctx_all[block], w_all[pl.ds(at, wrows), cols], preferred_element_type=jnp.float32
+            )
             acc[:, cols] = value + (residual[:, cols].astype(jnp.float32) if first else acc[:, cols])
 
     def add_blocks(step):
@@ -720,18 +770,14 @@
 
         lax.fori_loop(0, 2, way, 0)
 
-    ahead = takes[chunks:]
-    per = (len(rest) + len(ahead) - 1) // len(ahead)
-    for i, group_of in enumerate(ahead):
-        for take in group_of:
-            take_line(*take)
-        advance(rest[i * per : (i + 1) * per])
+    for jobs in due[heads:]:
+        advance(jobs)
     for d in range(m):
         finish(first_w + d)
     out_proj(t, True)
     for step in range(m - 1):
         if step == m - 2:
-            for chunk in range(chunks):
+            for chunk in range(heads):
                 take_line(step, chunk)
         add_blocks(step)
 
@@ -742,11 +788,14 @@
     for item in range(len(items)):
         drain(item)
     for f in order[1:]:
-        swap(f, False).wait_send()
+
+        @pl.when(far(f))
+        def _():
+            swap(f, False).wait_send()
 
     for step in range(m - 1):
         for cond, way, block, target in line_sends(m, t, step):
-            for chunk in range(chunks):
+            for chunk in range(heads):
 
                 @pl.when(cond)
                 def _():
@@ -757,12 +806,11 @@
     final.wait()
 
 
-def attend_and_mix(n, m, q, kv, pos, tokens, w_out, w_mix):
+def attend_and_mix(n, m, q, kv, pos, tokens, w_out, w_mix, w_near):
     heads, rows, _ = q.shape
     kv_heads = kv.shape[0]
     wrows, wcols = w_out.shape
     outs = tokens.shape[1]
-    chunks = heads // PAIR
     items = kv_heads + 1 + m
     bf16, f32 = jnp.bfloat16, jnp.float32
     dma = pltpu.SemaphoreType.DMA
@@ -772,12 +820,12 @@
             jax.ShapeDtypeStruct(tokens.shape, bf16),
             jax.ShapeDtypeStruct((rows, heads * HD), bf16),
         ),
-        in_specs=[VMEM, VMEM, VMEM, ANY, ANY, ANY],
+        in_specs=[VMEM, VMEM, VMEM, ANY, ANY, ANY, ANY],
         out_specs=(ANY, ANY),
         scratch_shapes=[
             pltpu.VMEM((kv_heads, n * rows, 2 * HD), bf16),
             pltpu.VMEM((n, *pos.shape), pos.dtype),
-            pltpu.VMEM((m, chunks, rows, PAIR * HD), bf16),
+            pltpu.VMEM((m, rows, heads * HD), bf16),
             pltpu.VMEM((m * wrows, outs), bf16),
             pltpu.VMEM((n, rows, rows), f32),
             pltpu.VMEM((rows, 128), f32),
@@ -788,15 +836,16 @@
             dma((items, plane_sems(n))),
             dma((m,)),
             dma((m,)),
-            dma((2, m - 1, chunks)),
-            dma((2, m - 1, chunks)),
-            dma((2 + chunks,)),
+            dma((2, m - 1, heads)),
+            dma((2, m - 1, heads)),
+            dma((2,)),
+            dma((2 + heads,)),
         ],
         compiler_params=pltpu.CompilerParams(
             collective_id=1, has_side_effects=True, vmem_limit_bytes=60 * 2**20
         ),
         cost_estimate=pl.CostEstimate(flops=10**11, bytes_accessed=10**8, transcendentals=0),
-    )(q, kv, pos, tokens, w_out, w_mix)
+    )(q, kv, pos, tokens, w_out, w_mix, w_near)
 
 
 def shards(seq, tensor, tokens, positions, norm_gain, w_query, w_key, w_value, b_query, b_key, b_value, w_out):
@@ -805,12 +854,12 @@
     inv_freq = ROPE_BASE ** (-jnp.arange(half, dtype=jnp.float32) * 2.0 / HD)
     inv_freq = jnp.concatenate((inv_freq, inv_freq))
     pos = jnp.broadcast_to(positions[None, :], (16, rows))
-    q, kv, w_mix = project(
+    q, kv, w_mix, w_near = project(
         seq, tensor, tokens, w_query, w_key, w_value, w_out,
         norm_gain.reshape(tensor, feats // w_query.shape[0], 1, w_query.shape[0]),
         b_query[None, :], b_key[None, :], b_value[None, :], positions[None, :], inv_freq[None, :],
     )
-    return attend_and_mix(seq, tensor, q, kv, pos, tokens, w_out, w_mix)
+    return attend_and_mix(seq, tensor, q, kv, pos, tokens, w_out, w_mix, w_near)
 
 
 def solution(mesh):

time: 282 us -> 274 us (0.972)
  Pallas kernels: 274 us -> 267 us
    pallas_call x1, Pallas kernels: 127 us -> 120 us  [attend_and_mix(): pl.pallas_call(functools.partial(attend_kernel, n, m), out_shape=(jax.Sha...]
where the time goes in v2:
time: 274 us; the launch traced here: 273 us
  Pallas kernels  267 us (97%)
  local copies, waits for them, and re-layouts  5.52 us (2%)
    pallas_call x1, Pallas kernels, project(): pl.pallas_call(functools.partial(project_kernel, n, m), out_shape=(jax.Sh...  147 us
    pallas_call x1, Pallas kernels, attend_and_mix(): pl.pallas_call(functools.partial(attend_kernel, n, m), out_shape=(jax.Sha...  120 us

profile of v2, /device:TPU:0, one launch (start us, length us, event | category | flops | bytes accessed | tf_op | source)
XLA Modules:
  0.0 273.5 jit_solution(12421455736973705564)
XLA Ops:
  0.6 0.6 maximum_bitcast_fusion.inv_freq
  1.2 1.3 broadcast_in_dim.26.pos
  2.5 146.6 %shard_map.113 = (bf16[8,512,128]{2,1,0:T(8,128)(2,1)}, bf16[2,512,256]{2,1,0:T(8,128)(2,1)}, bf16[4,256,1024]{2,1,0:T(8,128)(2,1)}, bf16[2,256,1024]{2,1,0:T(8,128)(2,1)}) custom-call(bf16[512,2048]{1,0:T(8,128)(2,1)} %tokens.3, bf16[1024,1024]{1,0:T(8,128)(2,1)} %w_query.1, bf16[1024,256]{1,0:T(8,128)(2,1)} %w_key.1, bf16[1024,256]{1,0:T(8,128)(2,1)} %w_value.1, ...), custom_call_target="tpu_custom_call" | custom-call | flops 99999997952 | bytes 100000000 | tf_op jit(solution)/shard_map/pallas_call | solution.py:460
  149.1 120.1 %shard_map.114 = (bf16[512,2048]{1,0:T(8,128)(2,1)}, bf16[512,1024]{1,0:T(8,128)(2,1)}) custom-call(bf16[8,512,128]{2,1,0:T(8,128)(2,1)} %get-tuple-element.6.q, bf16[2,512,256]{2,1,0:T(8,128)(2,1)} %get-tuple-element.7.kv, s32[16,512]{1,0:T(8,128)} %broadcast_in_dim.26.pos, bf16[512,2048]{1,0:T(8,128)(2,1)} %tokens.3, bf16[1024,1024]{1,0:T(8,128)(2,1)} %w_out.3, ...), custom_call_target="tpu_custom_call" | custom-call | flops 99999997952 | bytes 100000000 | tf_op jit(solution)/shard_map/pallas_call | solution.py:817
  269.2 0.0 copy-start
  269.3 3.2 %copy.14 = bf16[512,2048]{1,0:T(8,128)(2,1)} copy(bf16[512,2048]{1,0:T(8,128)(2,1)} %get-tuple-element.12) | data formatting | bytes 4194304
  272.5 0.0 copy-done
  272.5 1.0 copy.15
  (1 shorter events, 0.0 us)
Async XLA Ops:
  269.2 3.3 %copy-start = (bf16[512,1024]{1,0:T(8,128)(2,1)S(1)}, bf16[512,1024]{1,0:T(8,128)(2,1)}, u32[]{:S(2)}) copy-start(bf16[512,1024]{1,0:T(8,128)(2,1)} %get-tuple-element.13) | copy-start | bytes 3145732
